TPU v7x, 32 devices: a whole 2x2x4 slice. The times are simulated.
32 devices in a mesh: lat: 8 (over z, y), ch: 4 (over x, core).
Axes of the slice: x: 2, y: 2, z: 4, core: 2. Of those that a mesh axis runs over, the one named last changes fastest.
Arguments:
- field: bfloat16 [728, 256, 1440], P('lat', 'ch'), may hold values from -6 to 6
- legendre: bfloat16 [384, 721, 728], P(('lat', 'ch')), may hold values from -0.21875 to 0.21875
- pair_order: int32 [384], replicated, may hold values from 0 to 383, each once
Outputs:
- coeffs: float32 [384, 721, 2, 256], P(('lat', 'ch'))
Inputs may be any that keep to these rules, and one draw needn't show every extreme that they name: `pair_order`: each of 0 to 383 appears once; a value p below 360 gives its bin the orders p and 719 - p, and a bin with a larger value is empty.
All inputs are finite; a program needn't handle non-finite values.
Results may differ from a plain program's by a relative error of at most 0.0037.
Values may be sent and summed in bfloat16 or wider, within the bound.
A program may use at most 256 MiB of HBM per device.

v0:
```python
import math
import jax
import jax.numpy as jnp
from jax import lax
from jax.sharding import PartitionSpec as P

NLAT = 721
GROUPS = 4


def dft_table(points, modes, lon_count):
    columns = jnp.repeat(modes, 2)
    phase = jnp.tile(jnp.array([0, lon_count // 4], jnp.int32), modes.shape[0])
    turns = (points[:, None] * columns[None, :] + phase[None, :]) % lon_count
    angle = turns.astype(jnp.float32) * (2.0 * math.pi / lon_count)
    return jnp.cos(angle).astype(jnp.bfloat16)


def per_device(field, legendre, pair_order):
    lat_rows, chan_dev, lon_count = field.shape
    own, row_count, _ = legendre.shape
    lat_count = lax.axis_size("lat")
    ch_count = lax.axis_size("ch")
    dev_count = lat_count * ch_count
    me = lax.axis_index("lat") * ch_count + lax.axis_index("ch")
    max_order = row_count - 1
    keep_all = pair_order < max_order // 2
    first_order = jnp.where(keep_all, pair_order, 0)
    orders = jnp.stack([first_order, max_order - 1 - first_order], axis=1)
    bound_own = lax.dynamic_slice_in_dim(max_order - first_order, me * own, own)
    keep_own = lax.dynamic_slice_in_dim(keep_all, me * own, own)
    rows_global = lax.axis_index("lat") * lat_rows + jnp.arange(lat_rows, dtype=jnp.int32)
    in_grid = (rows_global < NLAT)[:, None, None]
    norm_scale = 2.0 * math.pi / lon_count
    points = jnp.arange(lon_count, dtype=jnp.int32)
    degree = jnp.arange(row_count, dtype=jnp.int32)
    groups = math.gcd(GROUPS, own)
    width = own // groups
    by_dev = orders.reshape(dev_count, own, 2)
    outs = []
    for g in range(groups):
        part = by_dev[:, g * width : (g + 1) * width].reshape(-1)
        basis = dft_table(points, part, lon_count)
        fourier = jnp.einsum("ack,kn->anc", field, basis, preferred_element_type=jnp.float32)
        fourier = jnp.where(in_grid, fourier * norm_scale, 0.0).astype(jnp.bfloat16)
        fourier = fourier.reshape(lat_rows, dev_count * width, 4 * chan_dev)
        got = lax.all_to_all(fourier, ("lat", "ch"), split_axis=1, concat_axis=0, tiled=True)
        got = got.reshape(lat_count, ch_count, lat_rows, width, 4, chan_dev)
        got = got.transpose(3, 0, 2, 4, 1, 5)
        got = got.reshape(width, lat_count * lat_rows, 4 * ch_count * chan_dev)
        products = jnp.einsum(
            "brl,bln->brn",
            legendre[g * width : (g + 1) * width],
            got,
            preferred_element_type=jnp.float32,
        )
        bound = bound_own[g * width : (g + 1) * width]
        keep = keep_own[g * width : (g + 1) * width]
        upper = degree[None, :, None] < bound[:, None, None]
        half = products.shape[2] // 2
        chosen = jnp.where(upper, products[:, :, :half], products[:, :, half:])
        chosen = chosen * keep[:, None, None].astype(jnp.float32)
        outs.append(chosen.reshape(width, row_count, 2, half // 2))
    return outs[0] if groups == 1 else jnp.concatenate(outs, axis=0)


def solution(mesh):
    in_specs = (P("lat", "ch", None), P(("lat", "ch"), None, None), P())
    out_specs = P(("lat", "ch"), None, None, None)
    return jax.shard_map(
        per_device, mesh=mesh, in_specs=in_specs, out_specs=out_specs, check_vma=False
    )
```

profile of v0, /device:TPU:0, one launch (start us, length us, event | category | flops | bytes accessed | tf_op | source)
XLA Modules:
  0.0 631.1 jit_solution(3836355545497258501)
XLA Ops:
  1.8 41.2 %fusion.8 = bf16[91,384,64]{1,0,2:T(8,128)(2,1)} fusion(pred[91]{0:T(512)(128)(4,1)S(1)} %add_compare_fusion, bf16[91,64,1440]{2,1,0:T(8,128)(2,1)} %param.7, s32[384]{0:T(512)S(1)} %add.79, s32[384]{0:T(512)S(1)} %mul.134), kind=kOutput, calls=%fused_computation.13 | convolution fusion | flops 6453669888 | bytes 21249116 | tf_op jit(solution)/shard_map/ack,kn->anc/dot_general | solution.py:44
  42.9 8.6 %copy.44 = bf16[91,384,64]{0,2,1:T(8,128)(2,1)} copy(bf16[91,384,64]{1,0,2:T(8,128)(2,1)} %fusion.8) | data formatting | bytes 8945664 | tf_op jit(solution)/shard_map/convert_element_type | solution.py:45
  51.5 8.3 %copy.45 = bf16[91,96,256]{2,0,1:T(8,128)(2,1)} copy(bf16[91,96,256]{0,2,1:T(8,128)(2,1)} %bitcast.80) | data formatting | bytes 8945664 | tf_op jit(solution)/shard_map/reshape | solution.py:46
  59.8 7.7 %all-to-all-start = ((bf16[91,96,256]{2,0,1:T(8,128)(2,1)}), bf16[91,96,256]{2,0,1:T(8,128)(2,1)}, u32[]{:S(2)}, u32[]{:S(2)}) async-start(bf16[91,96,256]{2,0,1:T(8,128)(2,1)} %copy.45), calls=%async_computation | async-start | bytes 9437184 | tf_op jit(solution)/shard_map/all_to_all | solution.py:47
  68.1 41.2 %fusion.9 = bf16[91,384,64]{1,0,2:T(8,128)(2,1)} fusion(pred[91]{0:T(512)(128)(4,1)S(1)} %add_compare_fusion, bf16[91,64,1440]{2,1,0:T(8,128)(2,1)} %param.7, s32[384]{0:T(512)S(1)} %mul.142, s32[384]{0:T(512)S(1)} %add.79), kind=kOutput, calls=%fused_computation.14 | convolution fusion | flops 6453669888 | bytes 21249116 | tf_op jit(solution)/shard_map/ack,kn->anc/dot_general | solution.py:44
  109.3 8.6 %copy.51 = bf16[91,384,64]{0,2,1:T(8,128)(2,1)} copy(bf16[91,384,64]{1,0,2:T(8,128)(2,1)} %fusion.9) | data formatting | bytes 8945664 | tf_op jit(solution)/shard_map/convert_element_type | solution.py:45
  117.9 8.3 %copy.52 = bf16[91,96,256]{2,0,1:T(8,128)(2,1)} copy(bf16[91,96,256]{0,2,1:T(8,128)(2,1)} %bitcast.81) | data formatting | bytes 8945664 | tf_op jit(solution)/shard_map/reshape | solution.py:46
  126.2 46.4 %all-to-all-done = bf16[91,96,256]{2,0,1:T(8,128)(2,1)} async-done(((bf16[91,96,256]{2,0,1:T(8,128)(2,1)}), bf16[91,96,256]{2,0,1:T(8,128)(2,1)}, u32[]{:S(2)}, u32[]{:S(2)}) %all-to-all-start) | async-done | bytes 4472864 | tf_op jit(solution)/shard_map/all_to_all | solution.py:47
  177.7 41.3 %fusion.10 = bf16[91,384,64]{1,0,2:T(8,128)(2,1)} fusion(pred[91]{0:T(512)(128)(4,1)S(1)} %add_compare_fusion, bf16[91,64,1440]{2,1,0:T(8,128)(2,1)} %param.7, s32[384]{0:T(512)S(1)} %mul.150, s32[384]{0:T(512)S(1)} %add.79), kind=kOutput, calls=%fused_computation.15 | convolution fusion | flops 6453669888 | bytes 21249116 | tf_op jit(solution)/shard_map/ack,kn->anc/dot_general | solution.py:44
  219.0 8.6 %copy.58 = bf16[91,384,64]{0,2,1:T(8,128)(2,1)} copy(bf16[91,384,64]{1,0,2:T(8,128)(2,1)} %fusion.10) | data formatting | bytes 8945664 | tf_op jit(solution)/shard_map/convert_element_type | solution.py:45
  227.6 8.3 %copy.59 = bf16[91,96,256]{2,0,1:T(8,128)(2,1)} copy(bf16[91,96,256]{0,2,1:T(8,128)(2,1)} %bitcast.82) | data formatting | bytes 8945664 | tf_op jit(solution)/shard_map/reshape | solution.py:46
  235.9 46.4 %all-to-all-done.1 = bf16[91,96,256]{2,0,1:T(8,128)(2,1)} async-done(((bf16[91,96,256]{2,0,1:T(8,128)(2,1)}), bf16[91,96,256]{2,0,1:T(8,128)(2,1)}, u32[]{:S(2)}, u32[]{:S(2)}) %all-to-all-start.1) | async-done | bytes 4472864 | tf_op jit(solution)/shard_map/all_to_all | solution.py:47
  287.1 41.2 %fusion.11 = bf16[91,384,64]{1,0,2:T(8,128)(2,1)} fusion(pred[91]{0:T(512)(128)(4,1)S(1)} %add_compare_fusion, bf16[91,64,1440]{2,1,0:T(8,128)(2,1)} %param.7, s32[384]{0:T(512)S(1)} %mul.158, s32[384]{0:T(512)S(1)} %add.79), kind=kOutput, calls=%fused_computation.16 | convolution fusion | flops 6453669888 | bytes 21249116 | tf_op jit(solution)/shard_map/ack,kn->anc/dot_general | solution.py:44
  328.3 8.6 %copy.65 = bf16[91,384,64]{0,2,1:T(8,128)(2,1)} copy(bf16[91,384,64]{1,0,2:T(8,128)(2,1)} %fusion.11) | data formatting | bytes 8945664 | tf_op jit(solution)/shard_map/convert_element_type | solution.py:45
  336.9 8.3 %copy.66 = bf16[91,96,256]{2,0,1:T(8,128)(2,1)} copy(bf16[91,96,256]{0,2,1:T(8,128)(2,1)} %bitcast.83) | data formatting | bytes 8945664 | tf_op jit(solution)/shard_map/reshape | solution.py:46
  345.2 46.4 %all-to-all-done.2 = bf16[91,96,256]{2,0,1:T(8,128)(2,1)} async-done(((bf16[91,96,256]{2,0,1:T(8,128)(2,1)}), bf16[91,96,256]{2,0,1:T(8,128)(2,1)}, u32[]{:S(2)}, u32[]{:S(2)}) %all-to-all-start.2) | async-done | bytes 4472864 | tf_op jit(solution)/shard_map/all_to_all | solution.py:47
  396.3 8.2 %copy.46 = bf16[32,91,3,256]{1,3,2,0:T(8,128)(2,1)} copy(bf16[32,91,3,256]{3,1,2,0:T(8,128)(2,1)} %bitcast.4) | data formatting | bytes 8945664 | tf_op jit(solution)/shard_map/all_to_all | solution.py:47
  404.6 18.3 %copy.47 = bf16[3,8,91,4,4,64]{2,1,5,4,3,0:T(8,128)(2,1)} copy(bf16[3,8,91,4,4,64]{2,5,3,0,4,1:T(8,128)(2,1)} %bitcast.76) | data formatting | bytes 8945664 | tf_op jit(solution)/shard_map/transpose | solution.py:49
  422.9 10.7 %reshape.217 = bf16[3,728,1024]{1,2,0:T(8,128)(2,1)} reshape(bf16[3,8,91,4,4,64]{2,1,5,4,3,0:T(8,128)(2,1)} %copy.47) | data formatting | bytes 8945664 | tf_op jit(solution)/shard_map/reshape | solution.py:50
  433.6 8.1 %copy.53 = bf16[32,91,3,256]{1,3,2,0:T(8,128)(2,1)} copy(bf16[32,91,3,256]{3,1,2,0:T(8,128)(2,1)} %bitcast.12) | data formatting | bytes 8945664 | tf_op jit(solution)/shard_map/all_to_all | solution.py:47
  441.6 18.1 %copy.54 = bf16[3,8,91,4,4,64]{2,1,5,4,3,0:T(8,128)(2,1)} copy(bf16[3,8,91,4,4,64]{2,5,3,0,4,1:T(8,128)(2,1)} %bitcast.77) | data formatting | bytes 8945664 | tf_op jit(solution)/shard_map/transpose | solution.py:49
  459.7 10.7 %reshape.219 = bf16[3,728,1024]{1,2,0:T(8,128)(2,1)} reshape(bf16[3,8,91,4,4,64]{2,1,5,4,3,0:T(8,128)(2,1)} %copy.54) | data formatting | bytes 8945664 | tf_op jit(solution)/shard_map/reshape | solution.py:50
  500.2 8.2 %copy.60 = bf16[32,91,3,256]{1,3,2,0:T(8,128)(2,1)} copy(bf16[32,91,3,256]{3,1,2,0:T(8,128)(2,1)} %bitcast.20) | data formatting | bytes 8945664 | tf_op jit(solution)/shard_map/all_to_all | solution.py:47
  508.5 18.4 %copy.61 = bf16[3,8,91,4,4,64]{2,1,5,4,3,0:T(8,128)(2,1)} copy(bf16[3,8,91,4,4,64]{2,5,3,0,4,1:T(8,128)(2,1)} %bitcast.78) | data formatting | bytes 8945664 | tf_op jit(solution)/shard_map/transpose | solution.py:49
  526.9 10.7 %reshape.221 = bf16[3,728,1024]{1,2,0:T(8,128)(2,1)} reshape(bf16[3,8,91,4,4,64]{2,1,5,4,3,0:T(8,128)(2,1)} %copy.61) | data formatting | bytes 8945664 | tf_op jit(solution)/shard_map/reshape | solution.py:50
  537.5 10.5 %fusion.30 = f32[3,721,1024]{2,1,0:T(8,128)} fusion(bf16[3,728,1024]{1,2,0:T(8,128)(2,1)} %reshape.221, bf16[12,721,728]{2,1,0:T(8,128)(2,1)} %param.8), kind=kOutput, calls=%fused_computation.35 | convolution fusion | flops 3224911872 | bytes 16932864 | tf_op jit(solution)/shard_map/brl,bln->brn/dot_general | solution.py:51
  548.1 8.1 %copy.67 = bf16[32,91,3,256]{1,3,2,0:T(8,128)(2,1)} copy(bf16[32,91,3,256]{3,1,2,0:T(8,128)(2,1)} %bitcast.28) | data formatting | bytes 8945664 | tf_op jit(solution)/shard_map/all_to_all | solution.py:47
  556.1 18.1 %copy.68 = bf16[3,8,91,4,4,64]{2,1,5,4,3,0:T(8,128)(2,1)} copy(bf16[3,8,91,4,4,64]{2,5,3,0,4,1:T(8,128)(2,1)} %bitcast.79) | data formatting | bytes 8945664 | tf_op jit(solution)/shard_map/transpose | solution.py:49
  574.3 10.8 %reshape.223 = bf16[3,728,1024]{1,2,0:T(8,128)(2,1)} reshape(bf16[3,8,91,4,4,64]{2,1,5,4,3,0:T(8,128)(2,1)} %copy.68) | data formatting | bytes 8945664 | tf_op jit(solution)/shard_map/reshape | solution.py:50
  585.0 10.8 %fusion.33 = f32[3,721,1024]{2,1,0:T(8,128)} fusion(bf16[3,728,1024]{1,2,0:T(8,128)(2,1)} %reshape.223, bf16[12,721,728]{2,1,0:T(8,128)(2,1)} %param.8), kind=kOutput, calls=%fused_computation.36 | convolution fusion | flops 3224911872 | bytes 16932864 | tf_op jit(solution)/shard_map/brl,bln->brn/dot_general | solution.py:51
  595.8 8.4 %fusion.12 = (f32[3,721,512]{2,1,0:T(8,128)}, f32[3,721,512]{2,1,0:T(8,128)}) fusion(f32[3,721,1024]{2,1,0:T(8,128)} %fusion.33, f32[3]{0:T(128)S(1)} %get-tuple-element.17, pred[3,721]{1,0:T(4,128)(4,1)S(1)} %iota_compare_fusion, f32[3]{0:T(128)S(1)} %get-tuple-element.18, f32[3,721,1024]{2,1,0:T(8,128)S(1)} %bitcast.85, ...), kind=kLoop, calls=%fused_computation.18 | loop fusion | flops 4429824 | bytes 26583294 | tf_op jit(solution)/shard_map/mul | solution.py:62
  617.0 13.8 %pad_maximum_fusion = f32[12,721,2,256]{3,2,1,0:T(2,128)} fusion(f32[3,721,2,256]{3,2,1,0:T(2,128)} %reshape.211, f32[3,721,2,256]{3,2,1,0:T(2,128)} %reshape.206, f32[3,721,2,256]{3,2,1,0:T(2,128)} %reshape.201, f32[3,721,2,256]{3,2,1,0:T(2,128)} %reshape.196), kind=kLoop, calls=%fused_computation | loop fusion | flops 13289472 | bytes 35438592 | tf_op jit(solution)/shard_map/concatenate | solution.py:64
  (55 shorter events, 59.4 us)
Async XLA Ops:
  59.8 112.8 %all-to-all-start = ((bf16[91,96,256]{2,0,1:T(8,128)(2,1)}), bf16[91,96,256]{2,0,1:T(8,128)(2,1)}, u32[]{:S(2)}, u32[]{:S(2)}) async-start(bf16[91,96,256]{2,0,1:T(8,128)(2,1)} %copy.45), calls=%async_computation | async-start | bytes 9437184 | tf_op jit(solution)/shard_map/all_to_all | solution.py:47
  172.6 109.7 %all-to-all-start.1 = ((bf16[91,96,256]{2,0,1:T(8,128)(2,1)}), bf16[91,96,256]{2,0,1:T(8,128)(2,1)}, u32[]{:S(2)}, u32[]{:S(2)}) async-start(bf16[91,96,256]{2,0,1:T(8,128)(2,1)} %copy.52), calls=%async_computation.1 | async-start | bytes 9437184 | tf_op jit(solution)/shard_map/all_to_all | solution.py:47
  282.3 109.3 %all-to-all-start.2 = ((bf16[91,96,256]{2,0,1:T(8,128)(2,1)}), bf16[91,96,256]{2,0,1:T(8,128)(2,1)}, u32[]{:S(2)}, u32[]{:S(2)}) async-start(bf16[91,96,256]{2,0,1:T(8,128)(2,1)} %copy.59), calls=%async_computation.2 | async-start | bytes 9437184 | tf_op jit(solution)/shard_map/all_to_all | solution.py:47
  345.2 50.6 %copy-start = (s32[384]{0:T(512)S(1)}, s32[384]{0:T(512)}, u32[]{:S(2)}) copy-start(s32[384]{0:T(512)} %param.9) | copy-start | bytes 4612
  391.6 156.5 %all-to-all-start.3 = ((bf16[91,96,256]{2,0,1:T(8,128)(2,1)}), bf16[91,96,256]{2,0,1:T(8,128)(2,1)}, u32[]{:S(2)}, u32[]{:S(2)}) async-start(bf16[91,96,256]{2,0,1:T(8,128)(2,1)} %copy.66), calls=%async_computation.3 | async-start | bytes 9437184 | tf_op jit(solution)/shard_map/all_to_all | solution.py:47
  574.3 21.6 %slice-start = ((s8[8945664]{0:T(1024)(128)(4,1)}), s8[557056]{0:T(1024)(128)(4,1)S(1)}, s32[]{:S(2)}) async-start(s8[8945664]{0:T(1024)(128)(4,1)} %bitcast.84), calls=%async_computation.4 | async-start | bytes 1114112
  585.0 10.8 %slice-start.1 = ((s8[8945664]{0:T(1024)(128)(4,1)}), s8[4194304]{0:T(1024)(128)(4,1)S(1)}, s32[]{:S(2)}) async-start(s8[8945664]{0:T(1024)(128)(4,1)} %bitcast.84), calls=%async_computation.5 | async-start | bytes 8388608
  585.0 10.8 %slice-start.2 = ((s8[8945664]{0:T(1024)(128)(4,1)}), s8[4194304]{0:T(1024)(128)(4,1)S(1)}, s32[]{:S(2)}) async-start(s8[8945664]{0:T(1024)(128)(4,1)} %bitcast.84), calls=%async_computation.6 | async-start | bytes 8388608
where the time goes:
time: 641 us; the launch traced here: 631 us
  local copies, waits for them, and re-layouts  244 us (38%)
  matrix products  199 us (31%)
  waiting for transfers between devices  139 us (22%)
  other arithmetic  27.2 us (4%)
  starting transfers between devices  20.7 us (3%)
    dot_general x4, matrix products, per_device(): jnp.einsum('ack,kn->anc', field, basis, preferred_element_type=jnp.float32)  165 us
    all_to_all x4, waiting for transfers between devices, per_device(): lax.all_to_all(fourier, ('lat', 'ch'), split_axis=1, concat_axis=0, tiled...  139 us
    transpose x4, local copies, waits for them, and re-layouts, per_device(): got = got.transpose(3, 0, 2, 4, 1, 5)  72.9 us
    reshape x4, local copies, waits for them, and re-layouts, per_device(): got = got.reshape(width, lat_count * lat_rows, 4 * ch_count * chan_dev)  42.8 us
    dot_general x4, matrix products, per_device(): jnp.einsum('brl,bln->brn', legendre[g * width:(g + 1) * width], got, pref...  34.5 us
    convert_element_type x4, local copies, waits for them, and re-layouts, per_device(): fourier = jnp.where(in_grid, fourier * norm_scale, 0.0).astype(jnp.bfloat16)  34.4 us
    reshape x4, local copies, waits for them, and re-layouts, per_device(): fourier = fourier.reshape(lat_rows, dev_count * width, 4 * chan_dev)  33.2 us
    all_to_all x4, local copies, waits for them, and re-layouts, per_device(): lax.all_to_all(fourier, ('lat', 'ch'), split_axis=1, concat_axis=0, tiled...  32.6 us
  transfers between devices with their start and end apart: 4, of which 3 were waited for; matrix products, arithmetic and copies ran while one was open for 52% of the time, Pallas kernels for 0%

commit v1 on v0

--- a/solution.py
+++ b/solution.py
@@ -44,7 +44,15 @@
         fourier = jnp.einsum("ack,kn->anc", field, basis, preferred_element_type=jnp.float32)
         fourier = jnp.where(in_grid, fourier * norm_scale, 0.0).astype(jnp.bfloat16)
         fourier = fourier.reshape(lat_rows, dev_count * width, 4 * chan_dev)
-        got = lax.all_to_all(fourier, ("lat", "ch"), split_axis=1, concat_axis=0, tiled=True)
+        got = jnp.concatenate(
+            lax.all_to_all(
+                jnp.stack(jnp.split(fourier, lax.axis_size(("lat", "ch")), axis=1)),
+                ("lat", "ch"),
+                0,
+                0,
+            ),
+            axis=0,
+        )
         got = got.reshape(lat_count, ch_count, lat_rows, width, 4, chan_dev)
         got = got.transpose(3, 0, 2, 4, 1, 5)
         got = got.reshape(width, lat_count * lat_rows, 4 * ch_count * chan_dev)

time: 641 us -> 680 us (1.061)
  local copies, waits for them, and re-layouts: 244 us -> 394 us
  waiting for transfers between devices: 139 us -> 27.2 us
    unnamed x8 -> x140, local copies, waits for them, and re-layouts: 0.01 us -> 147 us
    all_to_all x4, waiting for transfers between devices: 139 us -> 27.2 us  [per_device(): lax.all_to_all(jnp.stack(jnp.split(fourier, lax.axis_size(('lat', 'ch')),...]
    another operation x0 -> x8, local copies, waits for them, and re-layouts: none -> 36 us  [per_device(): jnp.stack(jnp.split(fourier, lax.axis_size(('lat', 'ch')), axis=1))]
    reshape x4 -> x0, local copies, waits for them, and re-layouts: 33.2 us -> none  [per_device(): fourier = fourier.reshape(lat_rows, dev_count * width, 4 * chan_dev)]
  transfers between devices with their start and end apart: 4 -> 4, of which waited for: 3 -> 3; matrix products, arithmetic and copies ran while one was open for 52% -> 66% of each run, Pallas kernels for 0% -> 0%
where the time goes in v1:
time: 680 us; the launch traced here: 668 us
  local copies, waits for them, and re-layouts  394 us (58%)
  matrix products  199 us (29%)
  other arithmetic  27.2 us (4%)
  waiting for transfers between devices  27.2 us (4%)
  starting transfers between devices  20.5 us (3%)
    dot_general x4, matrix products, per_device(): jnp.einsum('ack,kn->anc', field, basis, preferred_element_type=jnp.float32)  165 us
    unnamed x140, local copies, waits for them, and re-layouts  147 us
    transpose x4, local copies, waits for them, and re-layouts, per_device(): got = got.transpose(3, 0, 2, 4, 1, 5)  72.4 us
    reshape x4, local copies, waits for them, and re-layouts, per_device(): got = got.reshape(width, lat_count * lat_rows, 4 * ch_count * chan_dev)  42.8 us
    another operation x8, local copies, waits for them, and re-layouts, per_device(): jnp.stack(jnp.split(fourier, lax.axis_size(('lat', 'ch')), axis=1))  36 us
    dot_general x4, matrix products, per_device(): jnp.einsum('brl,bln->brn', legendre[g * width:(g + 1) * width], got, pref...  34.5 us
    convert_element_type x4, local copies, waits for them, and re-layouts, per_device(): fourier = jnp.where(in_grid, fourier * norm_scale, 0.0).astype(jnp.bfloat16)  34.4 us
    all_to_all x4, local copies, waits for them, and re-layouts, per_device(): lax.all_to_all(jnp.stack(jnp.split(fourier, lax.axis_size(('lat', 'ch')),...  33 us
  transfers between devices with their start and end apart: 4, of which 3 were waited for; matrix products, arithmetic and copies ran while one was open for 66% of the time, Pallas kernels for 0%

profile of v1, /device:TPU:0, one launch (start us, length us, event | category | flops | bytes accessed | tf_op | source)
XLA Modules:
  0.0 668.3 jit_solution(9074618563427853704)
XLA Ops:
  1.8 41.2 %fusion.8 = bf16[91,384,64]{1,0,2:T(8,128)(2,1)} fusion(pred[91]{0:T(512)(128)(4,1)S(1)} %add_compare_fusion, bf16[91,64,1440]{2,1,0:T(8,128)(2,1)} %param.7, s32[384]{0:T(512)S(1)} %add.79, s32[384]{0:T(512)S(1)} %mul.134), kind=kOutput, calls=%fused_computation.13 | convolution fusion | flops 6453669888 | bytes 21249116 | tf_op jit(solution)/shard_map/ack,kn->anc/dot_general | solution.py:44
  43.0 8.6 %copy.36 = bf16[91,384,64]{0,2,1:T(8,128)(2,1)} copy(bf16[91,384,64]{1,0,2:T(8,128)(2,1)} %fusion.8) | data formatting | bytes 8945664 | tf_op jit(solution)/shard_map/convert_element_type | solution.py:45
  89.0 8.3 %copy.37 = bf16[32,91,3,256]{3,1,2,0:T(8,128)(2,1)} copy(bf16[32,91,3,256]{1,3,2,0:T(8,128)(2,1)} %constant_dynamic-update-slice_fusion) | data formatting | bytes 8945664 | tf_op jit(solution)/shard_map/stack | solution.py:49
  97.3 7.9 %all-to-all-start = ((bf16[32,91,3,256]{3,1,2,0:T(8,128)(2,1)}), bf16[32,91,3,256]{3,1,2,0:T(8,128)(2,1)}, u32[]{:S(2)}, u32[]{:S(2)}) async-start(bf16[32,91,3,256]{3,1,2,0:T(8,128)(2,1)} %copy.37), calls=%async_computation | async-start | bytes 9437184 | tf_op jit(solution)/shard_map/all_to_all | solution.py:48
  105.7 41.2 %fusion.9 = bf16[91,384,64]{1,0,2:T(8,128)(2,1)} fusion(pred[91]{0:T(512)(128)(4,1)S(1)} %add_compare_fusion, bf16[91,64,1440]{2,1,0:T(8,128)(2,1)} %param.7, s32[384]{0:T(512)S(1)} %mul.142, s32[384]{0:T(512)S(1)} %add.79), kind=kOutput, calls=%fused_computation.14 | convolution fusion | flops 6453669888 | bytes 21249116 | tf_op jit(solution)/shard_map/ack,kn->anc/dot_general | solution.py:44
  146.9 8.6 %copy.43 = bf16[91,384,64]{0,2,1:T(8,128)(2,1)} copy(bf16[91,384,64]{1,0,2:T(8,128)(2,1)} %fusion.9) | data formatting | bytes 8945664 | tf_op jit(solution)/shard_map/convert_element_type | solution.py:45
  192.9 8.3 %copy.44 = bf16[32,91,3,256]{3,1,2,0:T(8,128)(2,1)} copy(bf16[32,91,3,256]{1,3,2,0:T(8,128)(2,1)} %constant_dynamic-update-slice_fusion.32) | data formatting | bytes 8945664 | tf_op jit(solution)/shard_map/stack | solution.py:49
  201.7 8.6 %all-to-all-done = bf16[32,91,3,256]{3,1,2,0:T(8,128)(2,1)} async-done(((bf16[32,91,3,256]{3,1,2,0:T(8,128)(2,1)}), bf16[32,91,3,256]{3,1,2,0:T(8,128)(2,1)}, u32[]{:S(2)}, u32[]{:S(2)}) %all-to-all-start) | async-done | bytes 4472864 | tf_op jit(solution)/shard_map/all_to_all | solution.py:48
  214.5 41.2 %fusion.10 = bf16[91,384,64]{1,0,2:T(8,128)(2,1)} fusion(pred[91]{0:T(512)(128)(4,1)S(1)} %add_compare_fusion, bf16[91,64,1440]{2,1,0:T(8,128)(2,1)} %param.7, s32[384]{0:T(512)S(1)} %mul.150, s32[384]{0:T(512)S(1)} %add.79), kind=kOutput, calls=%fused_computation.15 | convolution fusion | flops 6453669888 | bytes 21249116 | tf_op jit(solution)/shard_map/ack,kn->anc/dot_general | solution.py:44
  255.7 8.6 %copy.50 = bf16[91,384,64]{0,2,1:T(8,128)(2,1)} copy(bf16[91,384,64]{1,0,2:T(8,128)(2,1)} %fusion.10) | data formatting | bytes 8945664 | tf_op jit(solution)/shard_map/convert_element_type | solution.py:45
  301.7 8.3 %copy.51 = bf16[32,91,3,256]{3,1,2,0:T(8,128)(2,1)} copy(bf16[32,91,3,256]{1,3,2,0:T(8,128)(2,1)} %constant_dynamic-update-slice_fusion.64) | data formatting | bytes 8945664 | tf_op jit(solution)/shard_map/stack | solution.py:49
  310.5 9.0 %all-to-all-done.1 = bf16[32,91,3,256]{3,1,2,0:T(8,128)(2,1)} async-done(((bf16[32,91,3,256]{3,1,2,0:T(8,128)(2,1)}), bf16[32,91,3,256]{3,1,2,0:T(8,128)(2,1)}, u32[]{:S(2)}, u32[]{:S(2)}) %all-to-all-start.1) | async-done | bytes 4472864 | tf_op jit(solution)/shard_map/all_to_all | solution.py:48
  323.9 41.2 %fusion.11 = bf16[91,384,64]{1,0,2:T(8,128)(2,1)} fusion(pred[91]{0:T(512)(128)(4,1)S(1)} %add_compare_fusion, bf16[91,64,1440]{2,1,0:T(8,128)(2,1)} %param.7, s32[384]{0:T(512)S(1)} %mul.158, s32[384]{0:T(512)S(1)} %add.79), kind=kOutput, calls=%fused_computation.16 | convolution fusion | flops 6453669888 | bytes 21249116 | tf_op jit(solution)/shard_map/ack,kn->anc/dot_general | solution.py:44
  365.0 8.6 %copy.57 = bf16[91,384,64]{0,2,1:T(8,128)(2,1)} copy(bf16[91,384,64]{1,0,2:T(8,128)(2,1)} %fusion.11) | data formatting | bytes 8945664 | tf_op jit(solution)/shard_map/convert_element_type | solution.py:45
  411.1 8.3 %copy.58 = bf16[32,91,3,256]{3,1,2,0:T(8,128)(2,1)} copy(bf16[32,91,3,256]{1,3,2,0:T(8,128)(2,1)} %constant_dynamic-update-slice_fusion.96) | data formatting | bytes 8945664 | tf_op jit(solution)/shard_map/stack | solution.py:49
  419.3 9.6 %all-to-all-done.2 = bf16[32,91,3,256]{3,1,2,0:T(8,128)(2,1)} async-done(((bf16[32,91,3,256]{3,1,2,0:T(8,128)(2,1)}), bf16[32,91,3,256]{3,1,2,0:T(8,128)(2,1)}, u32[]{:S(2)}, u32[]{:S(2)}) %all-to-all-start.2) | async-done | bytes 4472864 | tf_op jit(solution)/shard_map/all_to_all | solution.py:48
  433.6 8.4 %copy.38 = bf16[32,91,3,256]{1,3,2,0:T(8,128)(2,1)} copy(bf16[32,91,3,256]{3,1,2,0:T(8,128)(2,1)} %all-to-all-done) | data formatting | bytes 8945664 | tf_op jit(solution)/shard_map/all_to_all | solution.py:48
  442.1 18.1 %copy.39 = bf16[3,8,91,4,4,64]{2,1,5,4,3,0:T(8,128)(2,1)} copy(bf16[3,8,91,4,4,64]{2,5,3,0,4,1:T(8,128)(2,1)} %bitcast.576) | data formatting | bytes 8945664 | tf_op jit(solution)/shard_map/transpose | solution.py:57
  460.2 10.7 %reshape.197 = bf16[3,728,1024]{1,2,0:T(8,128)(2,1)} reshape(bf16[3,8,91,4,4,64]{2,1,5,4,3,0:T(8,128)(2,1)} %copy.39) | data formatting | bytes 8945664 | tf_op jit(solution)/shard_map/reshape | solution.py:58
  470.8 8.1 %copy.45 = bf16[32,91,3,256]{1,3,2,0:T(8,128)(2,1)} copy(bf16[32,91,3,256]{3,1,2,0:T(8,128)(2,1)} %all-to-all-done.1) | data formatting | bytes 8945664 | tf_op jit(solution)/shard_map/all_to_all | solution.py:48
  478.9 18.1 %copy.46 = bf16[3,8,91,4,4,64]{2,1,5,4,3,0:T(8,128)(2,1)} copy(bf16[3,8,91,4,4,64]{2,5,3,0,4,1:T(8,128)(2,1)} %bitcast.577) | data formatting | bytes 8945664 | tf_op jit(solution)/shard_map/transpose | solution.py:57
  497.0 10.7 %reshape.199 = bf16[3,728,1024]{1,2,0:T(8,128)(2,1)} reshape(bf16[3,8,91,4,4,64]{2,1,5,4,3,0:T(8,128)(2,1)} %copy.46) | data formatting | bytes 8945664 | tf_op jit(solution)/shard_map/reshape | solution.py:58
  537.5 8.4 %copy.52 = bf16[32,91,3,256]{1,3,2,0:T(8,128)(2,1)} copy(bf16[32,91,3,256]{3,1,2,0:T(8,128)(2,1)} %all-to-all-done.2) | data formatting | bytes 8945664 | tf_op jit(solution)/shard_map/all_to_all | solution.py:48
  545.9 18.1 %copy.53 = bf16[3,8,91,4,4,64]{2,1,5,4,3,0:T(8,128)(2,1)} copy(bf16[3,8,91,4,4,64]{2,5,3,0,4,1:T(8,128)(2,1)} %bitcast.578) | data formatting | bytes 8945664 | tf_op jit(solution)/shard_map/transpose | solution.py:57
  564.0 10.7 %reshape.201 = bf16[3,728,1024]{1,2,0:T(8,128)(2,1)} reshape(bf16[3,8,91,4,4,64]{2,1,5,4,3,0:T(8,128)(2,1)} %copy.53) | data formatting | bytes 8945664 | tf_op jit(solution)/shard_map/reshape | solution.py:58
  574.7 10.5 %fusion.30 = f32[3,721,1024]{2,1,0:T(8,128)} fusion(bf16[3,728,1024]{1,2,0:T(8,128)(2,1)} %reshape.201, bf16[12,721,728]{2,1,0:T(8,128)(2,1)} %param.8), kind=kOutput, calls=%fused_computation.35 | convolution fusion | flops 3224911872 | bytes 16932864 | tf_op jit(solution)/shard_map/brl,bln->brn/dot_general | solution.py:59
  585.2 8.1 %copy.59 = bf16[32,91,3,256]{1,3,2,0:T(8,128)(2,1)} copy(bf16[32,91,3,256]{3,1,2,0:T(8,128)(2,1)} %all-to-all-done.3) | data formatting | bytes 8945664 | tf_op jit(solution)/shard_map/all_to_all | solution.py:48
  593.3 18.2 %copy.60 = bf16[3,8,91,4,4,64]{2,1,5,4,3,0:T(8,128)(2,1)} copy(bf16[3,8,91,4,4,64]{2,5,3,0,4,1:T(8,128)(2,1)} %bitcast.579) | data formatting | bytes 8945664 | tf_op jit(solution)/shard_map/transpose | solution.py:57
  611.5 10.8 %reshape.203 = bf16[3,728,1024]{1,2,0:T(8,128)(2,1)} reshape(bf16[3,8,91,4,4,64]{2,1,5,4,3,0:T(8,128)(2,1)} %copy.60) | data formatting | bytes 8945664 | tf_op jit(solution)/shard_map/reshape | solution.py:58
  622.2 10.8 %fusion.33 = f32[3,721,1024]{2,1,0:T(8,128)} fusion(bf16[3,728,1024]{1,2,0:T(8,128)(2,1)} %reshape.203, bf16[12,721,728]{2,1,0:T(8,128)(2,1)} %param.8), kind=kOutput, calls=%fused_computation.36 | convolution fusion | flops 3224911872 | bytes 16932864 | tf_op jit(solution)/shard_map/brl,bln->brn/dot_general | solution.py:59
  633.0 8.3 %fusion.12 = (f32[3,721,512]{2,1,0:T(8,128)}, f32[3,721,512]{2,1,0:T(8,128)}) fusion(f32[3,721,1024]{2,1,0:T(8,128)} %fusion.33, f32[3]{0:T(128)S(1)} %get-tuple-element.17, pred[3,721]{1,0:T(4,128)(4,1)S(1)} %iota_compare_fusion, f32[3]{0:T(128)S(1)} %get-tuple-element.18, f32[3,721,1024]{2,1,0:T(8,128)S(1)} %bitcast.709, ...), kind=kLoop, calls=%fused_computation.18 | loop fusion | flops 4429824 | bytes 26583294 | tf_op jit(solution)/shard_map/mul | solution.py:70
  654.2 13.8 %pad_maximum_fusion = f32[12,721,2,256]{3,2,1,0:T(2,128)} fusion(f32[3,721,2,256]{3,2,1,0:T(2,128)} %reshape.191, f32[3,721,2,256]{3,2,1,0:T(2,128)} %reshape.187, f32[3,721,2,256]{3,2,1,0:T(2,128)} %reshape.183, f32[3,721,2,256]{3,2,1,0:T(2,128)} %reshape.179), kind=kLoop, calls=%fused_computation | loop fusion | flops 13289472 | bytes 35438592 | tf_op jit(solution)/shard_map/concatenate | solution.py:72
  (191 shorter events, 208.6 us)
Async XLA Ops:
  51.5 26.3 %copy-start = (bf16[91,384,64]{0,2,1:T(8,128)(2,1)S(1)}, bf16[91,384,64]{0,2,1:T(8,128)(2,1)}, u32[]{:S(2)}) copy-start(bf16[91,384,64]{0,2,1:T(8,128)(2,1)} %copy.36) | copy-start | bytes 13418500
  97.3 113.0 %all-to-all-start = ((bf16[32,91,3,256]{3,1,2,0:T(8,128)(2,1)}), bf16[32,91,3,256]{3,1,2,0:T(8,128)(2,1)}, u32[]{:S(2)}, u32[]{:S(2)}) async-start(bf16[32,91,3,256]{3,1,2,0:T(8,128)(2,1)} %copy.37), calls=%async_computation | async-start | bytes 9437184 | tf_op jit(solution)/shard_map/all_to_all | solution.py:48
  155.5 26.3 %copy-start.1 = (bf16[91,384,64]{0,2,1:T(8,128)(2,1)S(1)}, bf16[91,384,64]{0,2,1:T(8,128)(2,1)}, u32[]{:S(2)}) copy-start(bf16[91,384,64]{0,2,1:T(8,128)(2,1)} %copy.43) | copy-start | bytes 13418500
  210.2 109.3 %all-to-all-start.1 = ((bf16[32,91,3,256]{3,1,2,0:T(8,128)(2,1)}), bf16[32,91,3,256]{3,1,2,0:T(8,128)(2,1)}, u32[]{:S(2)}, u32[]{:S(2)}) async-start(bf16[32,91,3,256]{3,1,2,0:T(8,128)(2,1)} %copy.44), calls=%async_computation.1 | async-start | bytes 9437184 | tf_op jit(solution)/shard_map/all_to_all | solution.py:48
  264.3 26.3 %copy-start.2 = (bf16[91,384,64]{0,2,1:T(8,128)(2,1)S(1)}, bf16[91,384,64]{0,2,1:T(8,128)(2,1)}, u32[]{:S(2)}) copy-start(bf16[91,384,64]{0,2,1:T(8,128)(2,1)} %copy.50) | copy-start | bytes 13418500
  319.6 109.4 %all-to-all-start.2 = ((bf16[32,91,3,256]{3,1,2,0:T(8,128)(2,1)}), bf16[32,91,3,256]{3,1,2,0:T(8,128)(2,1)}, u32[]{:S(2)}, u32[]{:S(2)}) async-start(bf16[32,91,3,256]{3,1,2,0:T(8,128)(2,1)} %copy.51), calls=%async_computation.2 | async-start | bytes 9437184 | tf_op jit(solution)/shard_map/all_to_all | solution.py:48
  373.6 26.3 %copy-start.3 = (bf16[91,384,64]{0,2,1:T(8,128)(2,1)S(1)}, bf16[91,384,64]{0,2,1:T(8,128)(2,1)}, u32[]{:S(2)}) copy-start(bf16[91,384,64]{0,2,1:T(8,128)(2,1)} %copy.57) | copy-start | bytes 13418500
  419.3 13.8 %copy-start.4 = (s32[384]{0:T(512)S(1)}, s32[384]{0:T(512)}, u32[]{:S(2)}) copy-start(s32[384]{0:T(512)} %param.9) | copy-start | bytes 4612
  428.9 156.3 %all-to-all-start.3 = ((bf16[32,91,3,256]{3,1,2,0:T(8,128)(2,1)}), bf16[32,91,3,256]{3,1,2,0:T(8,128)(2,1)}, u32[]{:S(2)}, u32[]{:S(2)}) async-start(bf16[32,91,3,256]{3,1,2,0:T(8,128)(2,1)} %copy.58), calls=%async_computation.3 | async-start | bytes 9437184 | tf_op jit(solution)/shard_map/all_to_all | solution.py:48
  611.5 21.6 %slice-start = ((s8[8945664]{0:T(1024)(128)(4,1)}), s8[557056]{0:T(1024)(128)(4,1)S(1)}, s32[]{:S(2)}) async-start(s8[8945664]{0:T(1024)(128)(4,1)} %bitcast.708), calls=%async_computation.4 | async-start | bytes 1114112
  622.2 10.8 %slice-start.1 = ((s8[8945664]{0:T(1024)(128)(4,1)}), s8[4194304]{0:T(1024)(128)(4,1)S(1)}, s32[]{:S(2)}) async-start(s8[8945664]{0:T(1024)(128)(4,1)} %bitcast.708), calls=%async_computation.5 | async-start | bytes 8388608
  622.2 10.8 %slice-start.2 = ((s8[8945664]{0:T(1024)(128)(4,1)}), s8[4194304]{0:T(1024)(128)(4,1)S(1)}, s32[]{:S(2)}) async-start(s8[8945664]{0:T(1024)(128)(4,1)} %bitcast.708), calls=%async_computation.6 | async-start | bytes 8388608
